TPU v7x, 256 devices: a whole 4x4x8 slice. The times are simulated.
256 devices in a mesh: fft: 32 (over z, y), band: 8 (over x, core).
Axes of the slice: x: 4, y: 4, z: 8, core: 2. Of those that a mesh axis runs over, the one named last changes fastest.
Arguments:
- coefficients: bfloat16 [96, 737280], P('band', 'fft'), may hold values from -0.0390625 to 0.0390625
- occupations: float32 [96], P('band'), may hold values from 0.5 to 2
- columns: int32 [5120], P('fft'), may hold values from 0 to 5183
- counts: int32 [32], P('fft'), may hold values from 1 to 160, 2048 in all
- plane_slot: int32 [160], replicated, may hold values from -1 to 143, as said below
Outputs:
- density: float32 [160, 144, 144], P('fft', 'band')
Inputs may be any that keep to these rules, and one draw needn't show every extreme that they name: The counts sum to 2048, and one of them equals 160. `plane_slot`: every plane 0 .. 143 stands in exactly one slot; the other slots hold -1.
All inputs are finite; a program needn't handle non-finite values. No bound on the sum of `counts` on one device may be relied on, other than what follows from the above.
Results may differ from a plain program's by a relative error of at most 0.0095.
Values may be sent and summed in bfloat16 or wider, within the bound.
A program may use at most 192 MiB of HBM per device.

v0:
```python
import math

import jax
import jax.numpy as jnp
from jax import lax
from jax.sharding import PartitionSpec as P

N = 144
GB = 72


def sent_to_all(x, axis):
    copies = jnp.broadcast_to(x, (lax.axis_size(axis), *x.shape))
    return lax.all_to_all(copies, axis, split_axis=0, concat_axis=0, tiled=True)


def joined_along(blocks, dim):
    blocks = jnp.moveaxis(blocks, 0, dim)
    lengths = blocks.shape
    return blocks.reshape(*lengths[:dim], lengths[dim] * lengths[dim + 1], *lengths[dim + 2 :])


def gathered_copies(x, axis, dim):
    blocks = sent_to_all(x, axis)
    return joined_along(blocks, dim)


def cut_along(x, dim, devices):
    before, after = (x.shape[:dim], x.shape[dim + 1 :])
    return jnp.moveaxis(x.reshape(*before, devices, -1, *after), dim, 0)


def summed_on_arrival(x, axis, dim):
    blocks = cut_along(x, dim, lax.axis_size(axis))
    arrived = lax.all_to_all(blocks, axis, split_axis=0, concat_axis=0, tiled=True)
    return arrived.astype(jnp.float32).sum(axis=0)


def phase_pair(freq_count, positions, grid):
    freqs = jnp.arange(freq_count, dtype=jnp.int32) - freq_count // 2
    turns = jnp.mod(freqs[:, None] * positions[None, :], grid)
    angles = turns.astype(jnp.float32) * (2.0 * math.pi / grid)
    return (jnp.cos(angles), jnp.sin(angles))


def stick_table(plane_slot):
    valid_slot = (plane_slot >= 0).astype(jnp.float32)
    cosine, sine_part = phase_pair(GB, jnp.maximum(plane_slot, 0), N)
    cosine = cosine * valid_slot[None, :]
    sine_part = sine_part * valid_slot[None, :]
    upper_rows = jnp.concatenate([cosine, sine_part], axis=1)
    lower_rows = jnp.concatenate([-sine_part, cosine], axis=1)
    return jnp.concatenate([upper_rows, lower_rows], axis=0).astype(jnp.bfloat16)


def row_table():
    cosine, sine_part = phase_pair(GB, jnp.arange(N, dtype=jnp.int32), N)
    upper_rows = jnp.concatenate([cosine, sine_part], axis=1)
    lower_rows = jnp.concatenate([-sine_part, cosine], axis=1)
    return jnp.concatenate([upper_rows, lower_rows], axis=0).astype(jnp.bfloat16)


def column_table():
    cosine, sine_part = phase_pair(GB, jnp.arange(N, dtype=jnp.int32), N)
    return jnp.concatenate([cosine.T, sine_part.T], axis=0).astype(jnp.bfloat16)


def grid_squares(received, row_pick, col_pick, row_tab, col_tab):
    bands_here, parts, planes, slot_total = received.shape
    flat_rows = bands_here * parts * planes
    by_slot = received.reshape(flat_rows, slot_total).T
    weighted = by_slot[:, :, None] * col_pick[:, None, :]
    placed = jnp.dot(
        row_pick.T, weighted.reshape(slot_total, flat_rows * GB), preferred_element_type=jnp.float32
    )
    placed = placed.reshape(GB, bands_here, parts, planes, GB)
    g_plane = (
        jnp.transpose(placed, (1, 3, 0, 2, 4))
        .reshape(bands_here, planes, GB, 2 * GB)
        .astype(jnp.bfloat16)
    )
    half_way = jnp.einsum(
        "bpgk,kj->bpgj", g_plane, row_tab, preferred_element_type=jnp.float32
    ).astype(jnp.bfloat16)
    full_grid = jnp.einsum("xg,bpgj->bpxj", col_tab, half_way, preferred_element_type=jnp.float32)
    real_part = full_grid[:, :, :N, :N] - full_grid[:, :, N:, N:]
    imag_part = full_grid[:, :, N:, :N] + full_grid[:, :, :N, N:]
    return real_part * real_part + imag_part * imag_part


def shards(coefficients, occupations, columns, counts, plane_slot):
    bands_here = coefficients.shape[0]
    coefficients = coefficients.reshape(bands_here, -1, 2 * GB)
    sticks_here = coefficients.shape[1]
    slot_count = plane_slot.shape[0]
    total_bands = bands_here * lax.axis_size("band")
    plane_tab = stick_table(plane_slot)
    row_tab = row_table()
    col_tab = column_table()
    stick_place = jnp.arange(sticks_here, dtype=jnp.int32)
    live_here = (stick_place < counts[0]).astype(jnp.bfloat16)
    coefficients = coefficients * live_here[None, :, None]
    every_column = gathered_copies(columns, "fft", 0)
    freq_ids = jnp.arange(GB, dtype=jnp.int32)[None, :]
    row_pick = ((every_column // GB)[:, None] == freq_ids).astype(jnp.bfloat16)
    col_pick = ((every_column % GB)[:, None] == freq_ids).astype(jnp.bfloat16)
    weights = occupations / total_bands
    sticks = jnp.einsum("bsg,go->bos", coefficients, plane_tab, preferred_element_type=jnp.float32)
    outgoing = sticks.astype(jnp.bfloat16).reshape(
        coefficients.shape[0], 2, slot_count, sticks_here
    )
    squares = grid_squares(
        lax.all_to_all(outgoing, "fft", split_axis=2, concat_axis=3, tiled=True),
        row_pick,
        col_pick,
        row_tab,
        col_tab,
    )
    local_sum = jnp.einsum("b,bpxy->pxy", weights, squares)
    return summed_on_arrival(local_sum.astype(jnp.bfloat16), "band", 1)


def solution(mesh):
    placed = (P("band", "fft"), P("band"), P("fft"), P("fft"), P())
    return jax.shard_map(
        shards, mesh=mesh, in_specs=placed, out_specs=P("fft", "band", None), check_vma=False
    )
```

profile of v0, /device:TPU:1, one launch (start us, length us, event | category | flops | bytes accessed | tf_op | source)
XLA Modules:
  0.0 225.7 jit_solution(1587791177518162412)
XLA Ops:
  0.0 1.3 broadcast_in_dim.2
  1.3 12.0 %all-to-all-start = ((s32[32,1,160]{2,1,0:T(1,128)}), s32[32,1,160]{2,1,0:T(1,128)S(1)}, u32[]{:S(2)}, u32[]{:S(2)}) async-start(s32[32,1,160]{2,1,0:T(1,128)} %broadcast_in_dim.2), calls=%async_computation | async-start | bytes 65536 | tf_op jit(solution)/shard_map/all_to_all | solution.py:14
  13.4 0.7 broadcast_maximum_fusion
  14.0 0.7 compare_convert_fusion.1
  14.7 2.8 %reshape.90 = bf16[12,160,144]{2,1,0:T(8,128)(2,1)S(1)} reshape(bf16[12,23040]{1,0:T(8,128)(2,1)} %param.5) | data formatting | bytes 1105920 | tf_op jit(solution)/shard_map/reshape | solution.py:93
  18.2 0.4 fusion.48
  18.6 0.7 fusion.9
  19.3 0.8 reshape.91
  20.1 5.5 %copy.12 = bf16[12,2,160,160]{3,1,0,2:T(2,128)(2,1)} copy(bf16[12,2,160,160]{2,1,3,0:T(2,128)(2,1)S(1)} %reshape.91) | data formatting | bytes 2457600 | tf_op jit(solution)/shard_map/reshape | solution.py:109
  25.6 9.4 %all-to-all-start.1 = ((bf16[12,2,160,160]{3,1,0,2:T(2,128)(2,1)}), bf16[12,2,160,160]{3,1,0,2:T(2,128)(2,1)S(1)}, u32[]{:S(2)}, u32[]{:S(2)}) async-start(bf16[12,2,160,160]{3,1,0,2:T(2,128)(2,1)} %copy.12), calls=%async_computation.1 | async-start | bytes 3932160 | tf_op jit(solution)/shard_map/all_to_all | solution.py:113
  35.0 0.4 cosine_convert_fusion
  35.4 0.4 fusion.42
  35.8 0.3 divide_reduce_fusion
  36.1 0.1 div.18
  36.2 0.1 compare_reduce_fusion
  36.4 0.1 ne.75
  36.5 0.1 fusion.8
  36.6 43.7 %all-to-all-done.1 = bf16[12,2,160,160]{3,1,0,2:T(2,128)(2,1)S(1)} async-done(((bf16[12,2,160,160]{3,1,0,2:T(2,128)(2,1)}), bf16[12,2,160,160]{3,1,0,2:T(2,128)(2,1)S(1)}, u32[]{:S(2)}, u32[]{:S(2)}) %all-to-all-start.1) | async-done | bytes 1228832 | tf_op jit(solution)/shard_map/all_to_all | solution.py:113
  80.3 1.8 copy.14
  82.1 4.4 %reshape.92 = bf16[120,5120]{1,0:T(8,128)(2,1)S(1)} reshape(bf16[12,2,5,32,160]{4,3,2,1,0:T(8,128)(2,1)} %copy.14) | data formatting | bytes 2457600 | tf_op jit(solution)/shard_map/reshape | solution.py:71
  86.5 27.5 %broadcast_multiply_fusion = bf16[5120,120,72]{0,2,1:T(8,128)(2,1)} fusion(bf16[5120,72]{0,1:T(8,128)(2,1)S(1)} %fusion.8, bf16[5120,120]{0,1:T(8,128)(2,1)S(1)} %bitcast.55), kind=kLoop, calls=%fused_computation | loop fusion | flops 44236800 | bytes 90439680 | tf_op jit(solution)/shard_map/mul | solution.py:72
  114.0 52.0 %convert_bitcast_fusion = bf16[12,5,72,2,72]{4,2,1,3,0:T(8,128)(2,1)S(1)} fusion(bf16[12,2,5,72,5120]{4,3,2,1,0:T(8,128)(2,1)} %bitcast.13, s32[5120]{0:T(1024)S(1)} %get-tuple-element.7), kind=kOutput, calls=%fused_computation.9 | convolution fusion | flops 6371089920 | bytes 89738240 | tf_op jit(solution)/shard_map/dot_general | solution.py:73
  166.1 2.4 %copy.15 = bf16[12,5,72,2,72]{2,4,3,1,0:T(8,128)(2,1)} copy(bf16[12,5,72,2,72]{4,2,1,3,0:T(8,128)(2,1)S(1)} %convert_bitcast_fusion) | data formatting | bytes 2488320 | tf_op jit(solution)/shard_map/convert_element_type | solution.py:80
  168.4 12.9 %convolution_bitcast_fusion = f32[12,5,288,288]{2,3,1,0:T(8,128)} fusion(bf16[12,5,72,144]{2,3,1,0:T(8,128)(2,1)} %bitcast.53, bf16[72,144]{1,0:T(8,128)(2,1)S(1)} %get-tuple-element.16, bf16[72,144]{1,0:T(8,128)(2,1)S(1)} %get-tuple-element.15, bf16[72,144]{1,0:T(8,128)(2,1)S(1)} %get-tuple-element.14, bf16[144,72]{0,1:T(8,128)(2,1)S(1)} %get-tuple-element.13, ...), kind=kOutput, calls=%fused_computation.1 | convolution fusion | flops 1076613120 | bytes 21254400 | tf_op jit(solution)/shard_map/xg,bpgj->bpxj/dot_general | solution.py:85
  181.3 15.4 %fusion.1 = bf16[12,5,144,144]{2,3,1,0:T(8,128)(2,1)} fusion(f32[12,5,288,288]{2,3,1,0:T(8,128)} %convolution_bitcast_fusion), kind=kLoop, calls=%fused_computation.4 | loop fusion | flops 7464960 | bytes 22394880 | tf_op jit(solution)/shard_map/add | solution.py:88
  196.7 10.3 %copy.24 = bf16[12,5,144,144]{3,0,2,1:T(8,128)(2,1)} copy(bf16[12,5,144,144]{2,3,1,0:T(8,128)(2,1)} %fusion.1) | data formatting | bytes 4976640 | tf_op jit(solution)/shard_map/add | solution.py:88
  207.0 3.6 %fusion.51 = bf16[1,5,144,144]{3,0,2,1:T(2,128)(2,1)S(1)} fusion(bf16[12,5,144,144]{3,0,2,1:T(8,128)(2,1)} %copy.24, f32[12]{0:T(128)S(1)} %copy-done), kind=kOutput, calls=%fused_computation.77 | convolution fusion | flops 2488332 | bytes 2695728 | tf_op jit(solution)/shard_map/b,bpxy->pxy/dot_general | solution.py:119
  210.7 0.1 reshape.93
  210.8 0.5 reshape.103
  211.4 12.9 %all_to_all.26 = bf16[8,2,6480]{2,1,0:T(2,128)(2,1)S(1)} all-to-all(bf16[8,2,6480]{2,1,0:T(2,128)(2,1)S(1)} %reshape.103), channel_id=1, replica_groups=mesh['fft'=32,'band'=8] {'band'}, dimensions={0} | all-to-all | bytes 414720 | tf_op jit(solution)/shard_map/all_to_all | solution.py:35
  224.3 0.6 reshape.104
  224.9 0.7 convert_reduce_fusion
  (9 shorter events, 0.2 us)
Async XLA Ops:
  1.3 24.3 %all-to-all-start = ((s32[32,1,160]{2,1,0:T(1,128)}), s32[32,1,160]{2,1,0:T(1,128)S(1)}, u32[]{:S(2)}, u32[]{:S(2)}) async-start(s32[32,1,160]{2,1,0:T(1,128)} %broadcast_in_dim.2), calls=%async_computation | async-start | bytes 65536 | tf_op jit(solution)/shard_map/all_to_all | solution.py:14
  25.6 54.7 %all-to-all-start.1 = ((bf16[12,2,160,160]{3,1,0,2:T(2,128)(2,1)}), bf16[12,2,160,160]{3,1,0,2:T(2,128)(2,1)S(1)}, u32[]{:S(2)}, u32[]{:S(2)}) async-start(bf16[12,2,160,160]{3,1,0,2:T(2,128)(2,1)} %copy.12), calls=%async_computation.1 | async-start | bytes 3932160 | tf_op jit(solution)/shard_map/all_to_all | solution.py:113
  196.7 10.3 %copy-start = (f32[12]{0:T(128)S(1)}, f32[12]{0:T(128)}, u32[]{:S(2)}) copy-start(f32[12]{0:T(128)} %param.6) | copy-start | bytes 148
where the time goes:
time: 226 us
  matrix products  69.3 us (31%)
  other arithmetic  46.7 us (21%)
  waiting for transfers between devices  43.7 us (19%)
  local copies, waits for them, and re-layouts  30.8 us (14%)
  starting transfers between devices  21.4 us (9%)
  blocking collectives  12.9 us (6%)
    dot_general x1, matrix products, grid_squares(): jnp.dot(row_pick.T, weighted.reshape(slot_total, flat_rows * GB), preferr...  52 us
    all_to_all x1, waiting for transfers between devices, shards(): lax.all_to_all(outgoing, 'fft', split_axis=2, concat_axis=3, tiled=True)  43.7 us
    mul x1, other arithmetic, grid_squares(): weighted = by_slot[:, :, None] * col_pick[:, None, :]  27.5 us
    add x1, other arithmetic, grid_squares(): return real_part * real_part + imag_part * imag_part  15.4 us
    all_to_all x1, blocking collectives, summed_on_arrival(): lax.all_to_all(blocks, axis, split_axis=0, concat_axis=0, tiled=True)  12.9 us
    dot_general x1, matrix products, grid_squares(): jnp.einsum('xg,bpgj->bpxj', col_tab, half_way, preferred_element_type=jnp...  12.9 us
    all_to_all x1, starting transfers between devices, sent_to_all(): return lax.all_to_all(copies, axis, split_axis=0, concat_axis=0, tiled=True)  12 us
    add x1, local copies, waits for them, and re-layouts, grid_squares(): return real_part * real_part + imag_part * imag_part  10.3 us
  transfers between devices with their start and end apart: 2, of which 1 were waited for; matrix products, arithmetic and copies ran while one was open for 6% of the time, Pallas kernels for 0%

commit v1 on v0

v1 whole, which is shorter than its diff:
```python
import functools

import jax
import jax.numpy as jnp
import numpy as np
from jax import lax
from jax.experimental import pallas as pl
from jax.experimental.pallas import tpu as pltpu
from jax.sharding import PartitionSpec as P

N = 144
GB = 72
BANDS_HERE = 12
SLOTS = 160
PLANES = 5
NF = 32
NB = 8
Z, Y = 8, 4
PAIRS = 15
ROWS = 32
TILES = 40
KALL = TILES * 128
CHUNKS = 5
XB = N // NB
F32 = jnp.float32
BF16 = jnp.bfloat16
MESH = pl.DeviceIdType.MESH

NT = (((1,), (1,)), ((), ()))


def trig(freqs, positions):
    turns = np.mod(freqs[:, None] * positions[None, :], N)
    angles = turns * (2.0 * np.pi / N)
    return np.cos(angles), np.sin(angles)


def stick_rows():
    cosine, sine = trig(np.arange(GB) - GB // 2, np.arange(N))
    rows = np.zeros((2 * N, 256), np.float32)
    rows[:N, :GB] = cosine.T
    rows[:N, GB : 2 * GB] = -sine.T
    rows[N:, :GB] = sine.T
    rows[N:, GB : 2 * GB] = cosine.T
    return jnp.asarray(rows, BF16)


def row_table():
    cosine, sine = trig(np.arange(GB) - GB // 2, np.arange(N))
    table = np.zeros((2, 256, 6, 256), np.float32)
    for third in range(3):
        at = slice(third * GB, (third + 1) * GB)
        table[0, at, third * 2, :N] = cosine
        table[0, at, third * 2 + 1, :N] = sine
        table[1, at, third * 2, :N] = -sine
        table[1, at, third * 2 + 1, :N] = cosine
    return jnp.asarray(table.reshape(512, 1536), BF16)


def column_table():
    cosine, sine = trig(np.arange(GB) - GB // 2, np.arange(N))
    table = np.zeros((2, N, 6, 32), np.float32)
    for third in range(3):
        c, s = cosine[third::3].T, sine[third::3].T
        table[0, :, third * 2, :24] = c
        table[0, :, third * 2 + 1, :24] = -s
        table[1, :, third * 2, :24] = s
        table[1, :, third * 2 + 1, :24] = c
    return jnp.asarray(table.reshape(2 * N, 192), BF16)


SEND_ORDER = [4 * dz + dy for dz in (4, 3, 5, 2, 6, 1, 7, 0) for dy in (2, 1, 3, 0)]
SEND_ORDER = [o for o in SEND_ORDER if o]


def kernel(
    x_ref, psel_ref, cols_ref, counts_ref, occ_ref, trow_ref, rt_ref, ct_ref,
    out_ref,
    w_ref, xc_ref, send_ref, rec_ref, rem_ref, hm_ref, oht_ref, lhs_ref,
    g_ref, hs_ref, sum_ref, stage_ref, bsend_ref, brec_ref, tot_ref,
    ssem, rsem, bssem, brsem,
):
    me = lax.axis_index("fft")
    band = lax.axis_index("band")
    my_z, my_y = me // Y, lax.rem(me, Y)

    def peer(o):
        dz, dy = o // Y, o % Y
        return lax.rem(my_z + dz, Z) * Y + lax.rem(my_y + dy, Y)

    barrier = pltpu.get_barrier_semaphore()
    for o in range(1, NF):
        pl.semaphore_signal(barrier, inc=1, device_id=(peer(o), band), device_id_type=MESH)
    for o in range(1, NB):
        pl.semaphore_signal(
            barrier, inc=1, device_id=(me, lax.rem(band + o, NB)), device_id_type=MESH
        )

    chosen = lax.broadcasted_iota(jnp.int32, (NF * ROWS, 2 * N), 1) == psel_ref[...]
    base = jnp.dot(
        jnp.where(chosen, 1.0, 0.0).astype(BF16), trow_ref[...], preferred_element_type=F32
    )
    row = lax.broadcasted_iota(jnp.int32, (NF * ROWS, 256), 0)
    within = lax.rem(row, 16)
    for bg in range(3):
        keep = (within >= bg * 5) & (within < bg * 5 + 5)
        w_ref[:, bg * 256 : (bg + 1) * 256] = jnp.where(keep, base, 0.0).astype(BF16)

    xc_ref[...] = jnp.zeros_like(xc_ref)
    for bg in range(3):
        for b4 in range(4):
            first = (bg * 4 + b4) * SLOTS
            xc_ref[1 + b4, :, bg * 256 : bg * 256 + 144] = x_ref[first : first + 128, :]
            xc_ref[0, 32 * b4 : 32 * b4 + 32, bg * 256 : bg * 256 + 144] = x_ref[
                first + 128 : first + SLOTS, :
            ]

    lane = lax.broadcasted_iota(jnp.int32, (1, 128), 1)
    count = counts_ref[0]
    row32 = lax.broadcasted_iota(jnp.int32, (ROWS, 128), 0)

    def outgoing(c):
        is_rem = c == 0
        slot = jnp.where(is_rem, 128 + lax.rem(lane, 32), lane)
        live = jnp.where(slot < count, 1.0, 0.0)
        res = lax.dot_general(w_ref[...], xc_ref[c], NT, preferred_element_type=F32) * live
        col = cols_ref[pl.ds(jnp.minimum(c, 1), 1), :]
        gx = jnp.floor((col + 0.5) * (1.0 / GB))
        gy = col - gx * GB
        aux = jnp.where(row32 == 15, gx, jnp.where(row32 == 31, gy, 0.0))
        send_ref[c] = (res.reshape(NF, ROWS, 128) + aux[None]).astype(BF16)

    def block_copy(c, o):
        return pltpu.make_async_remote_copy(
            src_ref=send_ref.at[c, peer(o)],
            dst_ref=rec_ref.at[c, o],
            send_sem=ssem.at[c],
            recv_sem=rsem.at[c],
            device_id=(peer(o), band),
            device_id_type=MESH,
        )

    def all_blocks(c):
        return pltpu.make_async_remote_copy(
            src_ref=send_ref.at[c, pl.ds(1, NF - 1)],
            dst_ref=rec_ref.at[c, pl.ds(1, NF - 1)],
            send_sem=ssem.at[c],
            recv_sem=rsem.at[c],
            device_id=(peer(1), band),
            device_id_type=MESH,
        )

    outgoing(0)
    pl.semaphore_wait(barrier, NF - 1 + NB - 1)

    def send_chunk(c, carry):
        @pl.when(c > 0)
        def _():
            outgoing(c)

        for o in SEND_ORDER:
            block_copy(c, o).start()
        rec_ref[c, 0] = send_ref[c, me]
        return carry

    lax.fori_loop(0, CHUNKS, send_chunk, 0)

    sum_ref[...] = jnp.zeros_like(sum_ref)

    all_blocks(0).wait_recv()

    def shuffle(g, carry):
        tiles = [rec_ref[0, 4 * g + j].astype(F32) for j in range(4)]
        quarter = lax.broadcasted_iota(jnp.int32, (ROWS, 128), 1) // 32
        for b4 in range(4):
            done = jnp.zeros((ROWS, 128), F32)
            for j in range(4):
                shift = (32 * (j - b4)) % 128
                moved = tiles[j] if shift == 0 else pltpu.roll(tiles[j], shift, 1)
                done = jnp.where(quarter == j, moved, done)
            rem_ref[b4, g] = done.astype(BF16)
        return carry

    lax.fori_loop(0, 8, shuffle, 0)

    all_blocks(1).wait_recv()

    def picks(tile, o):
        at = pl.ds(pl.multiple_of(o * 128, 128), 128)
        values = tile.astype(F32)
        gx, gy = values[15:16], values[31:32]
        hi = jnp.floor((gx + 0.5) * (1.0 / 3.0))
        lo = (gx - 3.0 * hi) * GB + gy
        h = lax.broadcasted_iota(jnp.int32, (32, 128), 0).astype(F32)
        hm_ref[:, at] = jnp.where(h == hi, 1.0, 0.0).astype(BF16)
        k = lax.broadcasted_iota(jnp.int32, (256, 128), 0).astype(F32)
        oht_ref[:, at] = jnp.where(k == lo, 1.0, 0.0).astype(BF16)

    def main_picks(o, carry):
        picks(rec_ref[1, o], o)
        return carry

    def rem_picks(g, carry):
        picks(rem_ref[0, g], 32 + g)
        return carry

    lax.fori_loop(0, NF, main_picks, 0)
    lax.fori_loop(0, 8, rem_picks, 0)

    def spread(tile, o):
        at = pl.ds(pl.multiple_of(o * 128, 128), 128)
        values = tile.astype(F32)
        top, low = hm_ref[0:16, at], hm_ref[16:32, at]
        for part in range(2):
            for r in range(PAIRS):
                q = part * 16 + r
                line = jnp.broadcast_to(values[q : q + 1], (16, 128)).astype(BF16)
                m = (part * PAIRS + r) * 32
                lhs_ref[m : m + 16, at] = line * top
                lhs_ref[m + 16 : m + 32, at] = line * low

    def stage(b4, carry):
        @pl.when(b4 > 0)
        def _():
            all_blocks(1 + b4).wait_recv()

        def main_spread(o, c):
            spread(rec_ref[1 + b4, o], o)
            return c

        def rem_spread(g, c):
            spread(rem_ref[b4, g], 32 + g)
            return c

        lax.fori_loop(0, NF, main_spread, 0)
        lax.fori_loop(0, 8, rem_spread, 0)
        for part in range(2):
            placed = lax.dot_general(
                lhs_ref[part * 480 : (part + 1) * 480, :], oht_ref[...], NT,
                preferred_element_type=F32,
            )
            g_ref[:, part * 256 : (part + 1) * 256] = placed.astype(BF16)
        for block in range(6):
            half = jnp.dot(
                g_ref[...], rt_ref[:, block * 256 : (block + 1) * 256],
                preferred_element_type=F32,
            )
            hs_ref[:, block * 32 : (block + 1) * 32, :] = half.astype(BF16).reshape(
                PAIRS, 32, 256
            )
        for p in range(PLANES):
            total = sum_ref[p]
            for bg in range(3):
                wave = jnp.dot(ct_ref[...], hs_ref[bg * 5 + p], preferred_element_type=F32)
                re, im = wave[:N], wave[N:]
                total += (re * re + im * im) * occ_ref[bg * 4 + b4]
            sum_ref[p] = total
        return carry

    lax.fori_loop(0, 4, stage, 0)

    for j in range(NB):
        for p in range(PLANES):
            stage_ref[j, XB * p : XB * (p + 1), :] = sum_ref[p, XB * j : XB * (j + 1), :]
        stage_ref[j, 90:96, :] = jnp.zeros((6, 256), F32)
        bsend_ref[j] = stage_ref[j].astype(BF16)
    for o in range(1, NB):
        to = lax.rem(band + o, NB)
        pltpu.make_async_remote_copy(
            src_ref=bsend_ref.at[to],
            dst_ref=brec_ref.at[o],
            send_sem=bssem,
            recv_sem=brsem,
            device_id=(me, to),
            device_id_type=MESH,
        ).start()
    band_blocks = pltpu.make_async_remote_copy(
        src_ref=bsend_ref.at[pl.ds(1, NB - 1)],
        dst_ref=brec_ref.at[pl.ds(1, NB - 1)],
        send_sem=bssem,
        recv_sem=brsem,
        device_id=(me, lax.rem(band + 1, NB)),
        device_id_type=MESH,
    )
    total = stage_ref[band]
    band_blocks.wait_recv()
    for o in range(1, NB):
        total += brec_ref[o].astype(F32)
    tot_ref[...] = total
    for p in range(PLANES):
        out_ref[p] = tot_ref[XB * p : XB * (p + 1), :N]
    for c in range(CHUNKS):
        all_blocks(c).wait_send()
    band_blocks.wait_send()


def shards(coefficients, occupations, columns, counts, plane_slot):
    x = coefficients.reshape(BANDS_HERE * SLOTS, 2 * GB)
    slots = jnp.broadcast_to(plane_slot.reshape(NF, 1, 1, PLANES), (NF, 2, 3, PLANES))
    slots = jnp.where(slots >= 0, slots + jnp.array([0, N], jnp.int32)[None, :, None, None], -1)
    slots = jnp.pad(slots.reshape(NF, 2, PAIRS), ((0, 0), (0, 0), (0, 1)), constant_values=-1)
    psel = slots.reshape(NF * ROWS, 1)
    cols = columns.astype(F32)
    cols = jnp.stack([jnp.tile(cols[128:], 4), cols[:128]])
    weights = occupations / (BANDS_HERE * NB)
    vmem = pl.BlockSpec(memory_space=pltpu.VMEM)
    smem = pl.BlockSpec(memory_space=pltpu.SMEM)
    return pl.pallas_call(
        kernel,
        out_shape=jax.ShapeDtypeStruct((PLANES, XB, N), F32),
        in_specs=[vmem, vmem, vmem, smem, smem, vmem, vmem, vmem],
        out_specs=vmem,
        scratch_shapes=[
            pltpu.VMEM((NF * ROWS, 768), BF16),
            pltpu.VMEM((CHUNKS, 128, 768), BF16),
            pltpu.VMEM((CHUNKS, NF, ROWS, 128), BF16),
            pltpu.VMEM((CHUNKS, NF, ROWS, 128), BF16),
            pltpu.VMEM((4, 8, ROWS, 128), BF16),
            pltpu.VMEM((32, KALL), BF16),
            pltpu.VMEM((256, KALL), BF16),
            pltpu.VMEM((960, KALL), BF16),
            pltpu.VMEM((480, 512), BF16),
            pltpu.VMEM((PAIRS, 192, 256), BF16),
            pltpu.VMEM((PLANES, N, 256), F32),
            pltpu.VMEM((NB, 96, 256), F32),
            pltpu.VMEM((NB, 96, 256), BF16),
            pltpu.VMEM((NB, 96, 256), BF16),
            pltpu.VMEM((96, 256), F32),
            pltpu.SemaphoreType.DMA((CHUNKS,)),
            pltpu.SemaphoreType.DMA((CHUNKS,)),
            pltpu.SemaphoreType.DMA,
            pltpu.SemaphoreType.DMA,
        ],
        compiler_params=pltpu.CompilerParams(
            collective_id=0, has_side_effects=True, vmem_limit_bytes=60 * 1024 * 1024
        ),
    )(x, psel, cols, counts, weights, stick_rows(), row_table(), column_table())


def solution(mesh):
    placed = (P("band", "fft"), P("band"), P("fft"), P("fft"), P())
    return jax.shard_map(
        shards, mesh=mesh, in_specs=placed, out_specs=P("fft", "band", None), check_vma=False
    )
```

time: 226 us -> 75 us (0.33)
  matrix products: 69.3 us -> 0 us
  Pallas kernels: 0 us -> 63.9 us
  other arithmetic: 46.7 us -> 2.48 us
  waiting for transfers between devices: 43.7 us -> 0 us
  local copies, waits for them, and re-layouts: 30.8 us -> 7.72 us
  starting transfers between devices: 21.4 us -> 0 us
  blocking collectives: 12.9 us -> 0 us
    dot_general x4 -> x0, matrix products: 69.3 us -> none  [the longest x1 52 us: grid_squares(): jnp.dot(row_pick.T, weighted.reshape(slot_total, flat_rows * GB), preferr...]
    pallas_call x0 -> x1, Pallas kernels: none -> 63.9 us  [shards(): pl.pallas_call(kernel, out_shape=jax.ShapeDtypeStruct((PLANES, XB, N), F3...]
    all_to_all x2 -> x0, waiting for transfers between devices: 43.7 us -> none  [the longest x1 43.7 us: shards(): lax.all_to_all(outgoing, 'fft', split_axis=2, concat_axis=3, tiled=True)]
    mul x1 -> x0, other arithmetic: 27.5 us -> none  [grid_squares(): weighted = by_slot[:, :, None] * col_pick[:, None, :]]
    all_to_all x2 -> x0, starting transfers between devices: 21.4 us -> none  [the longest x1 12 us: sent_to_all(): return lax.all_to_all(copies, axis, split_axis=0, concat_axis=0, tiled=True)]
    add x1 -> x0, other arithmetic: 15.4 us -> none  [grid_squares(): return real_part * real_part + imag_part * imag_part]
    all_to_all x1 -> x0, blocking collectives: 12.9 us -> none  [summed_on_arrival(): lax.all_to_all(blocks, axis, split_axis=0, concat_axis=0, tiled=True)]
    add x1 -> x0, local copies, waits for them, and re-layouts: 10.3 us -> none  [grid_squares(): return real_part * real_part + imag_part * imag_part]
  transfers between devices with their start and end apart: 2 -> 0, of which waited for: 1 -> 0; matrix products, arithmetic and copies ran while one was open for 6% -> 0% of each run, Pallas kernels for 0% -> 0%
where the time goes in v1:
time: 75 us; the launch traced here: 74.8 us
  Pallas kernels  63.9 us (85%)
  local copies, waits for them, and re-layouts  7.72 us (10%)
  other arithmetic  2.48 us (3%)
    pallas_call x1, Pallas kernels, shards(): pl.pallas_call(kernel, out_shape=jax.ShapeDtypeStruct((PLANES, XB, N), F3...  63.9 us
    reshape x1, local copies, waits for them, and re-layouts, shards(): x = coefficients.reshape(BANDS_HERE * SLOTS, 2 * GB)  3.76 us
    unnamed x1, local copies, waits for them, and re-layouts  1.56 us

profile of v1, /device:TPU:1, one launch (start us, length us, event | category | flops | bytes accessed | tf_op | source)
XLA Modules:
  0.0 74.8 jit_solution(5277221864108257114)
XLA Ops:
  0.7 1.1 %broadcast_multiply_fusion.occ_ref = f32[12]{0:T(128)} fusion(f32[12]{0:T(128)} %param.10), kind=kLoop, calls=%fused_computation.5 | loop fusion | flops 12 | bytes 96 | tf_op jit(solution)/shard_map/div | solution.py:305
  1.8 0.7 convert_element_type.3
  2.5 0.1 stack_tile.3
  2.6 0.6 pad_maximum_fusion.cols_ref
  3.1 0.8 %broadcast_in_dim.22 = s32[32,5]{1,0:T(8,128)S(1)} reshape(s32[160]{0:T(256)} %param.13) | data formatting | bytes 1280 | tf_op jit(solution)/shard_map/broadcast_in_dim | solution.py:299
  3.9 0.1 copy.12
  4.0 0.1 copy.10
  4.1 0.1 copy.11
  4.3 0.1 copy.13
  4.4 0.1 add_select_fusion
  4.5 1.1 %reshape.15.psel_ref = s32[1024,1]{1,0:T(8,128)} reshape(s32[32,2,16]{2,1,0:T(2,128)S(1)} %pad.4) | data formatting | bytes 8192 | tf_op jit(solution)/shard_map/reshape | solution.py:302
  5.6 3.8 %reshape.13.x_ref = bf16[1920,144]{1,0:T(8,128)(2,1)} reshape(bf16[12,23040]{1,0:T(8,128)(2,1)} %param.9) | data formatting | bytes 1105920 | tf_op jit(solution)/shard_map/reshape | solution.py:298
  9.3 63.9 %shard_map.91 = f32[5,18,144]{2,1,0:T(8,128)} custom-call(bf16[1920,144]{1,0:T(8,128)(2,1)} %reshape.13.x_ref, s32[1024,1]{1,0:T(8,128)} %reshape.15.psel_ref, f32[2,128]{1,0:T(2,128)} %pad_maximum_fusion.cols_ref, s32[1]{0:T(128)S(6)} %copy.16.counts_ref, f32[12]{0:T(128)} %broadcast_multiply_fusion.occ_ref, bf16[288,256]{1,0:T(8,128)(2,1)} %constant.17.clone.trow_ref, ...), custom_call_target="tpu_custom_call" | custom-call | tf_op jit(solution)/shard_map/pallas_call | solution.py:308
  73.3 1.6 %copy.17 = f32[5,18,144]{2,1,0:T(8,128)} copy(f32[5,18,144]{2,1,0:T(8,128)} %shard_map.91) | data formatting | bytes 103680
  (10 shorter events, 0.1 us)

commit v2 on v1

v2 whole, which is shorter than its diff:
```python
import functools

import jax
import jax.numpy as jnp
import numpy as np
from jax import lax
from jax.experimental import pallas as pl
from jax.experimental.pallas import tpu as pltpu
from jax.sharding import PartitionSpec as P

N = 144
GB = 72
BANDS_HERE = 12
SLOTS = 160
PLANES = 5
NF = 32
NB = 8
Z, Y = 8, 4
PAIRS = 15
ROWS = 32
TILES = 40
KALL = TILES * 128
HI = 24
STEP = 4
STEPS = TILES // STEP
CHUNKS = 5
XB = N // NB
F32 = jnp.float32
BF16 = jnp.bfloat16
MESH = pl.DeviceIdType.MESH

NT = (((1,), (1,)), ((), ()))


def trig(freqs, positions):
    turns = np.mod(freqs[:, None] * positions[None, :], N)
    angles = turns * (2.0 * np.pi / N)
    return np.cos(angles), np.sin(angles)


def stick_rows():
    cosine, sine = trig(np.arange(GB) - GB // 2, np.arange(N))
    rows = np.zeros((2 * N, 256), np.float32)
    rows[:N, :GB] = cosine.T
    rows[:N, GB : 2 * GB] = -sine.T
    rows[N:, :GB] = sine.T
    rows[N:, GB : 2 * GB] = cosine.T
    return jnp.asarray(rows, BF16)


def row_table():
    cosine, sine = trig(np.arange(GB) - GB // 2, np.arange(N))
    table = np.zeros((2, 256, 6, 256), np.float32)
    for third in range(3):
        at = slice(third * GB, (third + 1) * GB)
        table[0, at, third * 2, :N] = cosine
        table[0, at, third * 2 + 1, :N] = sine
        table[1, at, third * 2, :N] = -sine
        table[1, at, third * 2 + 1, :N] = cosine
    return jnp.asarray(table.reshape(512, 1536), BF16)


def column_table():
    cosine, sine = trig(np.arange(GB) - GB // 2, np.arange(N))
    table = np.zeros((2, N, 6, HI), np.float32)
    for third in range(3):
        c, s = cosine[third::3].T, sine[third::3].T
        table[0, :, third * 2] = c
        table[0, :, third * 2 + 1] = -s
        table[1, :, third * 2] = s
        table[1, :, third * 2 + 1] = c
    return jnp.asarray(table.reshape(2 * N, 6 * HI), BF16)


FAR_ORDER = [4 * dz + dy for dz in (4, 3, 5, 2) for dy in (2, 1, 3, 0)]
NEAR_ORDER = [4 * dz + dy for dz in (6, 1, 7, 0) for dy in (2, 1, 3, 0)][:-1]


def iota(shape, dim):
    return lax.broadcasted_iota(jnp.int32, shape, dim)


def kernel(
    x_hbm, trow_hbm, rt_hbm, ct_hbm, cols_ref, slot_ref, counts_ref, occ_ref,
    out_ref,
    x_ref, trow_ref, rt_ref, ct_ref, xf_ref, xr_ref, chosen_ref, w_ref, xc_ref, aux_ref,
    send_ref, rec_ref, hm_ref, oh_ref, lhs_a, lhs_b, acc_ref,
    g_ref, hs_ref, sum_ref, stage_ref, bsend_ref, brec_ref, tot_ref,
    ldsem, ssem, rsem, bssem, brsem,
):
    me = lax.axis_index("fft")
    band = lax.axis_index("band")
    my_z, my_y = me // Y, lax.rem(me, Y)

    def peer(o):
        dz, dy = o // Y, o % Y
        return lax.rem(my_z + dz, Z) * Y + lax.rem(my_y + dy, Y)

    barrier = pltpu.get_barrier_semaphore()
    for o in range(1, NF):
        pl.semaphore_signal(barrier, inc=1, device_id=(peer(o), band), device_id_type=MESH)
    for o in range(1, NB):
        pl.semaphore_signal(
            barrier, inc=1, device_id=(me, lax.rem(band + o, NB)), device_id_type=MESH
        )

    loads = [
        pltpu.make_async_copy(src, dst, ldsem.at[i])
        for i, (src, dst) in enumerate(
            ((trow_hbm, trow_ref), (x_hbm, x_ref), (rt_hbm, rt_ref), (ct_hbm, ct_ref))
        )
    ]
    for load in loads:
        load.start()

    def choose(d, carry):
        shape = (ROWS, 2 * N)
        row = iota(shape, 0)
        within = lax.rem(row, 16)
        plane = jnp.where(within < PAIRS, lax.rem(within, PLANES), PLANES)
        index = jnp.full(shape, -1, jnp.int32)
        for p in range(PLANES):
            index = jnp.where(plane == p, slot_ref[d * PLANES + p], index)
        hit = (iota(shape, 1) - N * (row // 16) == index) & (index >= 0)
        chosen_ref[pl.ds(pl.multiple_of(d * ROWS, ROWS), ROWS), :] = jnp.where(
            hit, 1.0, 0.0
        ).astype(BF16)
        return carry

    lax.fori_loop(0, NF, choose, 0)
    loads[0].wait()
    base = jnp.dot(chosen_ref[...], trow_ref[...], preferred_element_type=F32)
    within = lax.rem(iota((NF * ROWS, 256), 0), 16)
    for bg in range(3):
        keep = (within >= bg * PLANES) & (within < bg * PLANES + PLANES)
        w_ref[:, bg * 256 : (bg + 1) * 256] = jnp.where(keep, base, 0.0).astype(BF16)

    shape = (SLOTS, 256)
    l = iota(shape, 1)
    r = lax.rem(l, 32)
    wanted = jnp.where(l < 128, 8 * lax.rem(l, 16) + l // 16, 128 + 8 * lax.rem(r, 4) + r // 4)
    order = jnp.where(iota(shape, 0) == wanted, 1.0, 0.0).astype(BF16)
    col = jnp.broadcast_to(cols_ref[...].astype(F32), (16, SLOTS))
    gx = jnp.floor((col + 0.5) * (1.0 / GB))
    gy = col - gx * GB
    natural = jnp.where(iota((16, SLOTS), 0) == 0, gx, gy).astype(BF16)
    ordered = jnp.dot(natural, order, preferred_element_type=F32)
    aux_ref[0] = ordered[0:8, 128:]
    aux_ref[1] = ordered[0:8, :128]

    loads[1].wait()

    def widen(g, carry):
        for t in range(9):
            at = pl.ds(pl.multiple_of(g * 1152 + t * 128, 128), 128)
            xf_ref[pl.ds(pl.multiple_of((g * 9 + t) * 16, 16), BANDS_HERE), :] = x_ref[
                :, at
            ].astype(F32)
        return carry

    lax.fori_loop(0, 20, widen, 0)
    lane20 = iota((20, 128), 1)
    for b in range(BANDS_HERE):
        bg, b4 = b // 4, b % 4
        tiles = [xf_ref[pl.ds(t * 16 + b, 20, 144), :] for t in range(9)]
        for t in range(8):
            if t == 0:
                first, second = tiles[0], tiles[1]
            else:
                second = pltpu.roll(tiles[t + 1], 128 - 16 * t, 1)
                first = jnp.where(
                    lane20 < 128 - 16 * t, pltpu.roll(tiles[t], 128 - 16 * t, 1), second
                )
            for e, value in enumerate((first, second)):
                lanes = slice(bg * 256 + e * 128, bg * 256 + e * 128 + 128)
                xc_ref[1 + b4, 16 * t : 16 * t + 16, lanes] = value[:16].astype(BF16)
                xr_ref[b4, 4 * t : 4 * t + 4, lanes] = value[16:20]
    for b4 in range(4):
        xc_ref[0, 32 * b4 : 32 * b4 + 32, :] = xr_ref[b4].astype(BF16)

    lane = iota((1, 128), 1)
    count = counts_ref[0]
    row32 = iota((ROWS, 128), 0)

    def outgoing(c):
        r = lax.rem(lane, 32)
        slot = jnp.where(
            c == 0, 128 + 8 * lax.rem(r, 4) + r // 4, 8 * lax.rem(lane, 16) + lane // 16
        )
        live = jnp.where(slot < count, 1.0, 0.0)
        res = lax.dot_general(w_ref[...], xc_ref[c], NT, preferred_element_type=F32) * live
        columns = aux_ref[jnp.minimum(c, 1)]
        aux = jnp.where(row32 == 15, columns[0:1], jnp.where(row32 == 31, columns[1:2], 0.0))
        send_ref[c] = (res.reshape(NF, ROWS, 128) + aux[None]).astype(BF16)

    def block_copy(c, o, half):
        return pltpu.make_async_remote_copy(
            src_ref=send_ref.at[c, peer(o)],
            dst_ref=rec_ref.at[c, o],
            send_sem=ssem.at[c],
            recv_sem=rsem.at[c, half],
            device_id=(peer(o), band),
            device_id_type=MESH,
        )

    def blocks(c, first, size, half):
        return pltpu.make_async_remote_copy(
            src_ref=send_ref.at[c, pl.ds(0, size)],
            dst_ref=rec_ref.at[c, pl.ds(first, size)],
            send_sem=ssem.at[c],
            recv_sem=rsem.at[c, half],
            device_id=(peer(1), band),
            device_id_type=MESH,
        )

    def wait_far(c):
        blocks(c, 8, 16, 0).wait_recv()

    def wait_near(c):
        blocks(c, 1, 15, 1).wait_recv()

    outgoing(0)
    pl.semaphore_wait(barrier, NF - 1 + NB - 1)

    def send_chunk(c, carry):
        @pl.when(c > 0)
        def _():
            outgoing(c)

        for o in FAR_ORDER:
            block_copy(c, o, 0).start()
        for o in NEAR_ORDER:
            block_copy(c, o, 1).start()
        rec_ref[c, 0] = send_ref[c, me]
        return carry

    lax.fori_loop(0, CHUNKS, send_chunk, 0)

    sum_ref[...] = jnp.zeros_like(sum_ref)

    wait_far(0)
    wait_near(0)

    def shuffle(g, carry):
        tiles = [rec_ref[0, 4 * g + j].astype(F32) for j in range(4)]
        quarter = iota((ROWS, 128), 1) // 32
        for b4 in range(4):
            done = jnp.zeros((ROWS, 128), F32)
            for j in range(4):
                shift = (32 * (j - b4)) % 128
                moved = tiles[j] if shift == 0 else pltpu.roll(tiles[j], shift, 1)
                done = jnp.where(quarter == j, moved, done)
            rec_ref[1 + b4, 32 + g] = done.astype(BF16)
        return carry

    lax.fori_loop(0, 8, shuffle, 0)

    wait_far(1)
    wait_near(1)

    def picks(o, carry):
        at = pl.ds(pl.multiple_of(o * 128, 128), 128)
        values = rec_ref[1, o].astype(F32)
        gx, gy = values[15:16], values[31:32]
        hi = jnp.floor((gx + 0.5) * (1.0 / 3.0))
        lo = (gx - 3.0 * hi) * GB + gy
        i = iota((48, 128), 0)
        h = jnp.where(i < 24, i, i - 24).astype(F32)
        hm_ref[:, at] = jnp.where(h == hi, 1.0, 0.0).astype(BF16)
        column = jnp.transpose(jnp.broadcast_to(lo, (8, 128)))[:, 0:1]
        k = iota((128, 256), 1).astype(F32)
        oh_ref[at, :] = jnp.where(k == column, 1.0, 0.0).astype(BF16)
        return carry

    lax.fori_loop(0, TILES, picks, 0)

    rows = [part * 16 + r for part in range(2) for r in range(PAIRS)]

    def first_tile(step):
        late = jnp.where(step < 8, 4 * step, 4 * step - 32)
        return jnp.where(step < 4, 8 + 4 * step, jnp.where(step < 6, 16 + 4 * step, late))

    def spread(b4, step, lhs_ref):
        for j in range(STEP):
            o = first_tile(step) + j
            at = pl.ds(pl.multiple_of(o * 128, 128), 128)
            values = rec_ref[1 + b4, o].astype(F32)
            picked = hm_ref[:, at]
            lanes = slice(j * 128, j * 128 + 128)
            for i in range(PAIRS):
                a = jnp.broadcast_to(values[rows[2 * i] : rows[2 * i] + 1], (8, 128))
                b = jnp.broadcast_to(values[rows[2 * i + 1] : rows[2 * i + 1] + 1], (8, 128))
                for e, pair in enumerate(((a, a), (a, b), (b, b))):
                    m = 48 * i + 16 * e
                    lhs_ref[m : m + 16, lanes] = (
                        jnp.concatenate(pair, axis=0).astype(BF16)
                        * picked[16 * e : 16 * e + 16]
                    )

    def place(step, lhs_ref, fresh):
        at = pl.ds(pl.multiple_of(first_tile(step) * 128, 128), STEP * 128)
        got = jnp.dot(lhs_ref[...], oh_ref[at, :], preferred_element_type=F32)
        acc_ref[...] = got if fresh else acc_ref[...] + got

    def stage(b4, carry):
        @pl.when(b4 > 0)
        def _():
            wait_far(1 + b4)

        spread(b4, 0, lhs_a)
        acc_ref[...] = jnp.zeros_like(acc_ref)

        def two(i, c):
            @pl.when((b4 > 0) & (i == 2))
            def _():
                wait_near(1 + b4)

            place(2 * i, lhs_a, False)
            spread(b4, 2 * i + 1, lhs_b)
            place(2 * i + 1, lhs_b, False)
            spread(b4, jnp.minimum(2 * i + 2, STEPS - 1), lhs_a)
            return c

        lax.fori_loop(0, STEPS // 2, two, 0)
        half_rows = PAIRS * HI
        g_ref[:, :256] = acc_ref[:half_rows].astype(BF16)
        g_ref[:, 256:] = acc_ref[half_rows:].astype(BF16)
        for block in range(6):
            half = jnp.dot(
                g_ref[...], rt_ref[:, block * 256 : (block + 1) * 256],
                preferred_element_type=F32,
            )
            hs_ref[:, block * HI : (block + 1) * HI, :] = half.reshape(PAIRS, HI, 256)
        for p in range(PLANES):
            total = sum_ref[p]
            for bg in range(3):
                wave = jnp.dot(
                    ct_ref[...], hs_ref[bg * PLANES + p].astype(BF16),
                    preferred_element_type=F32,
                )
                re, im = wave[:N], wave[N:]
                total += (re * re + im * im) * (occ_ref[bg * 4 + b4] * (1.0 / (BANDS_HERE * NB)))
            sum_ref[p] = total
        return carry

    loads[2].wait()
    loads[3].wait()
    lax.fori_loop(0, 4, stage, 0)

    folded = iota((16, 128), 1) // 16
    for j in range(NB):
        for p in range(PLANES):
            stage_ref[j, XB * p : XB * (p + 1), :] = sum_ref[p, XB * j : XB * (j + 1), :]
        stage_ref[j, 90:96, :] = jnp.zeros((6, 256), F32)
        extra = jnp.zeros((16, 128), F32)
        for i in range(6):
            piece = stage_ref[j, 16 * i : 16 * i + 16, 128:]
            if i:
                piece = pltpu.roll(piece, 16 * i, 1)
            extra = jnp.where(folded == i, piece, extra)
        bsend_ref[j, :96] = stage_ref[j, :, :128].astype(BF16)
        bsend_ref[j, 96:] = extra.astype(BF16)
    for o in range(1, NB):
        to = lax.rem(band + o, NB)
        pltpu.make_async_remote_copy(
            src_ref=bsend_ref.at[to],
            dst_ref=brec_ref.at[o],
            send_sem=bssem,
            recv_sem=brsem,
            device_id=(me, to),
            device_id_type=MESH,
        ).start()
    band_blocks = pltpu.make_async_remote_copy(
        src_ref=bsend_ref.at[pl.ds(1, NB - 1)],
        dst_ref=brec_ref.at[pl.ds(1, NB - 1)],
        send_sem=bssem,
        recv_sem=brsem,
        device_id=(me, lax.rem(band + 1, NB)),
        device_id_type=MESH,
    )
    total = bsend_ref[band].astype(F32)
    for c in range(CHUNKS):
        blocks(c, 0, NF - 1, 0).wait_send()
    band_blocks.wait_recv()
    for o in range(1, NB):
        total += brec_ref[o].astype(F32)
    tot_ref[:, :128] = total[:96]
    for i in range(6):
        piece = total[96:]
        if i:
            piece = pltpu.roll(piece, 128 - 16 * i, 1)
        tot_ref[16 * i : 16 * i + 16, 128:] = piece
    for p in range(PLANES):
        out_ref[p] = tot_ref[XB * p : XB * (p + 1), :N]
    band_blocks.wait_send()


def shards(coefficients, occupations, columns, counts, plane_slot):
    vmem = pl.BlockSpec(memory_space=pltpu.VMEM)
    smem = pl.BlockSpec(memory_space=pltpu.SMEM)
    hbm = pl.BlockSpec(memory_space=pl.ANY)
    rows = 2 * PAIRS * HI
    return pl.pallas_call(
        kernel,
        out_shape=jax.ShapeDtypeStruct((PLANES, XB, N), F32),
        in_specs=[hbm, hbm, hbm, hbm, vmem, smem, smem, smem],
        out_specs=vmem,
        scratch_shapes=[
            pltpu.VMEM((BANDS_HERE, SLOTS * 2 * GB), BF16),
            pltpu.VMEM((2 * N, 256), BF16),
            pltpu.VMEM((512, 1536), BF16),
            pltpu.VMEM((2 * N, 6 * HI), BF16),
            pltpu.VMEM((2880, 128), F32),
            pltpu.VMEM((4, 32, 768), F32),
            pltpu.VMEM((NF * ROWS, 2 * N), BF16),
            pltpu.VMEM((NF * ROWS, 768), BF16),
            pltpu.VMEM((CHUNKS, 128, 768), BF16),
            pltpu.VMEM((2, 8, 128), F32),
            pltpu.VMEM((CHUNKS, NF, ROWS, 128), BF16),
            pltpu.VMEM((CHUNKS, TILES, ROWS, 128), BF16),
            pltpu.VMEM((48, KALL), BF16),
            pltpu.VMEM((KALL, 256), BF16),
            pltpu.VMEM((rows, STEP * 128), BF16),
            pltpu.VMEM((rows, STEP * 128), BF16),
            pltpu.VMEM((rows, 256), F32),
            pltpu.VMEM((PAIRS * HI, 512), BF16),
            pltpu.VMEM((PAIRS, 6 * HI, 256), F32),
            pltpu.VMEM((PLANES, N, 256), F32),
            pltpu.VMEM((NB, 96, 256), F32),
            pltpu.VMEM((NB, 112, 128), BF16),
            pltpu.VMEM((NB, 112, 128), BF16),
            pltpu.VMEM((96, 256), F32),
            pltpu.SemaphoreType.DMA((4,)),
            pltpu.SemaphoreType.DMA((CHUNKS,)),
            pltpu.SemaphoreType.DMA((CHUNKS, 2)),
            pltpu.SemaphoreType.DMA,
            pltpu.SemaphoreType.DMA,
        ],
        compiler_params=pltpu.CompilerParams(
            collective_id=0, has_side_effects=True, vmem_limit_bytes=60 * 1024 * 1024
        ),
    )(
        coefficients, stick_rows(), row_table(), column_table(),
        columns.reshape(1, SLOTS), plane_slot, counts, occupations,
    )


def solution(mesh):
    placed = (P("band", "fft"), P("band"), P("fft"), P("fft"), P())
    return jax.shard_map(
        shards, mesh=mesh, in_specs=placed, out_specs=P("fft", "band", None), check_vma=False
    )
```

time: 75 us -> 60.5 us (0.81)
  local copies, waits for them, and re-layouts: 7.72 us -> 1.56 us
  Pallas kernels: 63.9 us -> 58.2 us
  other arithmetic: 2.48 us -> 0 us
    pallas_call x1, Pallas kernels: 63.9 us -> 58.2 us  [shards(): pl.pallas_call(kernel, out_shape=jax.ShapeDtypeStruct((PLANES, XB, N), F3...]
    reshape x2 -> x0, local copies, waits for them, and re-layouts: 4.88 us -> none  [the longest x1 3.76 us: shards(): x = coefficients.reshape(BANDS_HERE * SLOTS, 2 * GB)]
    div x1 -> x0, other arithmetic: 1.14 us -> none  [shards(): weights = occupations / (BANDS_HERE * NB)]
    broadcast_in_dim x8 -> x0, local copies, waits for them, and re-layouts: 1.07 us -> none  [shards(): jnp.broadcast_to(plane_slot.reshape(NF, 1, 1, PLANES), (NF, 2, 3, PLANES))]
where the time goes in v2:
time: 60.5 us; the launch traced here: 60.4 us
  Pallas kernels  58.2 us (96%)
  local copies, waits for them, and re-layouts  1.56 us (3%)
  between operations  0.66 us (1%)
    pallas_call x1, Pallas kernels, shards(): pl.pallas_call(kernel, out_shape=jax.ShapeDtypeStruct((PLANES, XB, N), F3...  58.2 us
    unnamed x1, local copies, waits for them, and re-layouts  1.56 us

profile of v2, /device:TPU:1, one launch (start us, length us, event | category | flops | bytes accessed | tf_op | source)
XLA Modules:
  0.0 60.4 jit_solution(7698321203958771474)
XLA Ops:
  0.7 58.2 %shard_map.82 = f32[5,18,144]{2,1,0:T(8,128)} custom-call(bf16[12,23040]{1,0:T(8,128)(2,1)} %x_hbm.1, bf16[288,256]{1,0:T(8,128)(2,1)} %constant.6.clone.trow_hbm, bf16[512,1536]{1,0:T(8,128)(2,1)} %constant.7.clone.rt_hbm, bf16[288,144]{1,0:T(8,128)(2,1)} %constant.8.clone.ct_hbm, s32[1,160]{1,0:T(1,128)} %bitcast.1, s32[160]{0:T(256)} %slot_ref.1, ...), custom_call_target="tpu_custom_call" | custom-call | tf_op jit(solution)/shard_map/pallas_call | solution.py:403
  58.8 1.6 %copy.11 = f32[5,18,144]{2,1,0:T(8,128)} copy(f32[5,18,144]{2,1,0:T(8,128)} %shard_map.82) | data formatting | bytes 103680

commit v3 on v2

--- a/solution.py
+++ b/solution.py
@@ -83,10 +83,10 @@
 def kernel(
     x_hbm, trow_hbm, rt_hbm, ct_hbm, cols_ref, slot_ref, counts_ref, occ_ref,
     out_ref,
-    x_ref, trow_ref, rt_ref, ct_ref, xf_ref, xr_ref, chosen_ref, w_ref, xc_ref, aux_ref,
+    x_ref, trow_ref, rt_ref, ct_ref, xf_ref, xr_ref, chosen_ref, w_ref, xc_ref, code_ref, codes_ref,
     send_ref, rec_ref, hm_ref, oh_ref, lhs_a, lhs_b, acc_ref,
     g_ref, hs_ref, sum_ref, stage_ref, bsend_ref, brec_ref, tot_ref,
-    ldsem, ssem, rsem, bssem, brsem,
+    ldsem, cssem, crsem, ssem, rsem, bssem, brsem,
 ):
     me = lax.axis_index("fft")
     band = lax.axis_index("band")
@@ -145,8 +145,7 @@
     gy = col - gx * GB
     natural = jnp.where(iota((16, SLOTS), 0) == 0, gx, gy).astype(BF16)
     ordered = jnp.dot(natural, order, preferred_element_type=F32)
-    aux_ref[0] = ordered[0:8, 128:]
-    aux_ref[1] = ordered[0:8, :128]
+    code_ref[...] = ordered[0:1] * GB + ordered[1:2]
 
     loads[1].wait()
 
@@ -180,7 +179,6 @@
 
     lane = iota((1, 128), 1)
     count = counts_ref[0]
-    row32 = iota((ROWS, 128), 0)
 
     def outgoing(c):
         r = lax.rem(lane, 32)
@@ -189,9 +187,7 @@
         )
         live = jnp.where(slot < count, 1.0, 0.0)
         res = lax.dot_general(w_ref[...], xc_ref[c], NT, preferred_element_type=F32) * live
-        columns = aux_ref[jnp.minimum(c, 1)]
-        aux = jnp.where(row32 == 15, columns[0:1], jnp.where(row32 == 31, columns[1:2], 0.0))
-        send_ref[c] = (res.reshape(NF, ROWS, 128) + aux[None]).astype(BF16)
+        send_ref[c] = res.reshape(NF, ROWS, 128).astype(BF16)
 
     def block_copy(c, o, half):
         return pltpu.make_async_remote_copy(
@@ -219,8 +215,21 @@
     def wait_near(c):
         blocks(c, 1, 15, 1).wait_recv()
 
+    def code_copy(o):
+        return pltpu.make_async_remote_copy(
+            src_ref=code_ref,
+            dst_ref=codes_ref.at[o],
+            send_sem=cssem,
+            recv_sem=crsem,
+            device_id=(peer(o), band),
+            device_id_type=MESH,
+        )
+
     outgoing(0)
     pl.semaphore_wait(barrier, NF - 1 + NB - 1)
+    for o in FAR_ORDER + NEAR_ORDER:
+        code_copy(o).start()
+    codes_ref[0] = code_ref[...]
 
     def send_chunk(c, carry):
         @pl.when(c > 0)
@@ -237,6 +246,41 @@
     lax.fori_loop(0, CHUNKS, send_chunk, 0)
 
     sum_ref[...] = jnp.zeros_like(sum_ref)
+
+    every_code = pltpu.make_async_remote_copy(
+        src_ref=codes_ref.at[pl.ds(1, NF - 1)],
+        dst_ref=codes_ref.at[pl.ds(1, NF - 1)],
+        send_sem=cssem,
+        recv_sem=crsem,
+        device_id=(peer(1), band),
+        device_id_type=MESH,
+    )
+    every_code.wait_recv()
+
+    def picks(o, code):
+        at = pl.ds(pl.multiple_of(o * 128, 128), 128)
+        hi = jnp.floor((code + 0.5) * (1.0 / (3 * GB)))
+        lo = code - 3 * GB * hi
+        i = iota((48, 128), 0)
+        h = jnp.where(i < 24, i, i - 24).astype(F32)
+        hm_ref[:, at] = jnp.where(h == hi, 1.0, 0.0).astype(BF16)
+        k = iota((256, 128), 0).astype(F32)
+        oh_ref[:, at] = jnp.where(k == lo, 1.0, 0.0).astype(BF16)
+
+    def main_picks(o, carry):
+        picks(o, codes_ref[o, :, :128])
+        return carry
+
+    def rem_picks(g, carry):
+        quarter = iota((1, 128), 1) // 32
+        code = codes_ref[4 * g, :, 128:]
+        for j in range(1, 4):
+            code = jnp.where(quarter == j, codes_ref[4 * g + j, :, 128:], code)
+        picks(32 + g, code)
+        return carry
+
+    lax.fori_loop(0, NF, main_picks, 0)
+    lax.fori_loop(0, 8, rem_picks, 0)
 
     wait_far(0)
     wait_near(0)
@@ -254,25 +298,6 @@
         return carry
 
     lax.fori_loop(0, 8, shuffle, 0)
-
-    wait_far(1)
-    wait_near(1)
-
-    def picks(o, carry):
-        at = pl.ds(pl.multiple_of(o * 128, 128), 128)
-        values = rec_ref[1, o].astype(F32)
-        gx, gy = values[15:16], values[31:32]
-        hi = jnp.floor((gx + 0.5) * (1.0 / 3.0))
-        lo = (gx - 3.0 * hi) * GB + gy
-        i = iota((48, 128), 0)
-        h = jnp.where(i < 24, i, i - 24).astype(F32)
-        hm_ref[:, at] = jnp.where(h == hi, 1.0, 0.0).astype(BF16)
-        column = jnp.transpose(jnp.broadcast_to(lo, (8, 128)))[:, 0:1]
-        k = iota((128, 256), 1).astype(F32)
-        oh_ref[at, :] = jnp.where(k == column, 1.0, 0.0).astype(BF16)
-        return carry
-
-    lax.fori_loop(0, TILES, picks, 0)
 
     rows = [part * 16 + r for part in range(2) for r in range(PAIRS)]
 
@@ -299,19 +324,16 @@
 
     def place(step, lhs_ref, fresh):
         at = pl.ds(pl.multiple_of(first_tile(step) * 128, 128), STEP * 128)
-        got = jnp.dot(lhs_ref[...], oh_ref[at, :], preferred_element_type=F32)
+        got = lax.dot_general(lhs_ref[...], oh_ref[:, at], NT, preferred_element_type=F32)
         acc_ref[...] = got if fresh else acc_ref[...] + got
 
     def stage(b4, carry):
-        @pl.when(b4 > 0)
-        def _():
-            wait_far(1 + b4)
-
+        wait_far(1 + b4)
         spread(b4, 0, lhs_a)
         acc_ref[...] = jnp.zeros_like(acc_ref)
 
         def two(i, c):
-            @pl.when((b4 > 0) & (i == 2))
+            @pl.when(i == 2)
             def _():
                 wait_near(1 + b4)
 
@@ -393,12 +415,13 @@
     for p in range(PLANES):
         out_ref[p] = tot_ref[XB * p : XB * (p + 1), :N]
     band_blocks.wait_send()
+    every_code.wait_send()
 
 
 def shards(coefficients, occupations, columns, counts, plane_slot):
     vmem = pl.BlockSpec(memory_space=pltpu.VMEM)
     smem = pl.BlockSpec(memory_space=pltpu.SMEM)
-    hbm = pl.BlockSpec(memory_space=pl.ANY)
+    hbm = pl.BlockSpec(memory_space=pltpu.HBM)
     rows = 2 * PAIRS * HI
     return pl.pallas_call(
         kernel,
@@ -415,11 +438,12 @@
             pltpu.VMEM((NF * ROWS, 2 * N), BF16),
             pltpu.VMEM((NF * ROWS, 768), BF16),
             pltpu.VMEM((CHUNKS, 128, 768), BF16),
-            pltpu.VMEM((2, 8, 128), F32),
+            pltpu.VMEM((1, 256), F32),
+            pltpu.VMEM((NF, 1, 256), F32),
             pltpu.VMEM((CHUNKS, NF, ROWS, 128), BF16),
             pltpu.VMEM((CHUNKS, TILES, ROWS, 128), BF16),
             pltpu.VMEM((48, KALL), BF16),
-            pltpu.VMEM((KALL, 256), BF16),
+            pltpu.VMEM((256, KALL), BF16),
             pltpu.VMEM((rows, STEP * 128), BF16),
             pltpu.VMEM((rows, STEP * 128), BF16),
             pltpu.VMEM((rows, 256), F32),
@@ -431,6 +455,8 @@
             pltpu.VMEM((NB, 112, 128), BF16),
             pltpu.VMEM((96, 256), F32),
             pltpu.SemaphoreType.DMA((4,)),
+            pltpu.SemaphoreType.DMA,
+            pltpu.SemaphoreType.DMA,
             pltpu.SemaphoreType.DMA((CHUNKS,)),
             pltpu.SemaphoreType.DMA((CHUNKS, 2)),
             pltpu.SemaphoreType.DMA,

time: 60.5 us -> 56.5 us (0.934)
  Pallas kernels: 58.2 us -> 54.1 us
    pallas_call x1, Pallas kernels: 58.2 us -> 54.1 us  [shards(): pl.pallas_call(kernel, out_shape=jax.ShapeDtypeStruct((PLANES, XB, N), F3...]
where the time goes in v3:
time: 56.5 us; the launch traced here: 56.3 us
  Pallas kernels  54.1 us (96%)
  local copies, waits for them, and re-layouts  1.56 us (3%)
  between operations  0.66 us (1%)
    pallas_call x1, Pallas kernels, shards(): pl.pallas_call(kernel, out_shape=jax.ShapeDtypeStruct((PLANES, XB, N), F3...  54.1 us
    unnamed x1, local copies, waits for them, and re-layouts  1.56 us

profile of v3, /device:TPU:1, one launch (start us, length us, event | category | flops | bytes accessed | tf_op | source)
XLA Modules:
  0.0 56.3 jit_solution(5383426962067073243)
XLA Ops:
  0.7 54.1 %shard_map.82 = f32[5,18,144]{2,1,0:T(8,128)} custom-call(bf16[12,23040]{1,0:T(8,128)(2,1)} %x_hbm.1, bf16[288,256]{1,0:T(8,128)(2,1)} %constant.6.clone.trow_hbm, bf16[512,1536]{1,0:T(8,128)(2,1)} %constant.7.clone.rt_hbm, bf16[288,144]{1,0:T(8,128)(2,1)} %constant.8.clone.ct_hbm, s32[1,160]{1,0:T(1,128)} %bitcast.1, s32[160]{0:T(256)} %slot_ref.1, ...), custom_call_target="tpu_custom_call" | custom-call | tf_op jit(solution)/shard_map/pallas_call | solution.py:426
  54.8 1.6 %copy.11 = f32[5,18,144]{2,1,0:T(8,128)} copy(f32[5,18,144]{2,1,0:T(8,128)} %shard_map.82) | data formatting | bytes 103680

commit v4 on v3

--- a/solution.py
+++ b/solution.py
@@ -21,8 +21,7 @@
 TILES = 40
 KALL = TILES * 128
 HI = 24
-STEP = 4
-STEPS = TILES // STEP
+STEP = 10
 CHUNKS = 5
 XB = N // NB
 F32 = jnp.float32
@@ -72,8 +71,7 @@
     return jnp.asarray(table.reshape(2 * N, 6 * HI), BF16)
 
 
-FAR_ORDER = [4 * dz + dy for dz in (4, 3, 5, 2) for dy in (2, 1, 3, 0)]
-NEAR_ORDER = [4 * dz + dy for dz in (6, 1, 7, 0) for dy in (2, 1, 3, 0)][:-1]
+ORDER = [Y * dz + dy for dz in (0, 4, 3, 5, 2, 6, 1, 7) for dy in range(Y)]
 
 
 def iota(shape, dim):
@@ -189,46 +187,46 @@
         res = lax.dot_general(w_ref[...], xc_ref[c], NT, preferred_element_type=F32) * live
         send_ref[c] = res.reshape(NF, ROWS, 128).astype(BF16)
 
-    def block_copy(c, o, half):
+    def block_copy(c, i):
         return pltpu.make_async_remote_copy(
-            src_ref=send_ref.at[c, peer(o)],
-            dst_ref=rec_ref.at[c, o],
+            src_ref=send_ref.at[c, peer(ORDER[i])],
+            dst_ref=rec_ref.at[c, i],
             send_sem=ssem.at[c],
-            recv_sem=rsem.at[c, half],
-            device_id=(peer(o), band),
+            recv_sem=rsem.at[c, i // 16 if i != 16 else 2],
+            device_id=(peer(ORDER[i]), band),
             device_id_type=MESH,
         )
 
-    def blocks(c, first, size, half):
+    def blocks(c, first, size, group):
         return pltpu.make_async_remote_copy(
             src_ref=send_ref.at[c, pl.ds(0, size)],
             dst_ref=rec_ref.at[c, pl.ds(first, size)],
             send_sem=ssem.at[c],
-            recv_sem=rsem.at[c, half],
+            recv_sem=rsem.at[c, group],
             device_id=(peer(1), band),
             device_id_type=MESH,
         )
 
-    def wait_far(c):
-        blocks(c, 8, 16, 0).wait_recv()
-
-    def wait_near(c):
-        blocks(c, 1, 15, 1).wait_recv()
-
-    def code_copy(o):
+    def wait_one(c):
+        blocks(c, 16, 1, 2).wait_recv()
+
+    def wait_group(c, group):
+        blocks(c, 1 + 16 * group, 15, group).wait_recv()
+
+    def code_copy(i):
         return pltpu.make_async_remote_copy(
             src_ref=code_ref,
-            dst_ref=codes_ref.at[o],
+            dst_ref=codes_ref.at[i],
             send_sem=cssem,
             recv_sem=crsem,
-            device_id=(peer(o), band),
+            device_id=(peer(ORDER[i]), band),
             device_id_type=MESH,
         )
 
     outgoing(0)
     pl.semaphore_wait(barrier, NF - 1 + NB - 1)
-    for o in FAR_ORDER + NEAR_ORDER:
-        code_copy(o).start()
+    for i in range(1, NF):
+        code_copy(i).start()
     codes_ref[0] = code_ref[...]
 
     def send_chunk(c, carry):
@@ -236,10 +234,8 @@
         def _():
             outgoing(c)
 
-        for o in FAR_ORDER:
-            block_copy(c, o, 0).start()
-        for o in NEAR_ORDER:
-            block_copy(c, o, 1).start()
+        for i in range(1, NF):
+            block_copy(c, i).start()
         rec_ref[c, 0] = send_ref[c, me]
         return carry
 
@@ -257,6 +253,8 @@
     )
     every_code.wait_recv()
 
+    identity = jnp.where(iota((128, 128), 0) == iota((128, 128), 1), 1.0, 0.0).astype(BF16)
+
     def picks(o, code):
         at = pl.ds(pl.multiple_of(o * 128, 128), 128)
         hi = jnp.floor((code + 0.5) * (1.0 / (3 * GB)))
@@ -265,25 +263,32 @@
         h = jnp.where(i < 24, i, i - 24).astype(F32)
         hm_ref[:, at] = jnp.where(h == hi, 1.0, 0.0).astype(BF16)
         k = iota((256, 128), 0).astype(F32)
-        oh_ref[:, at] = jnp.where(k == lo, 1.0, 0.0).astype(BF16)
-
-    def main_picks(o, carry):
-        picks(o, codes_ref[o, :, :128])
-        return carry
-
-    def rem_picks(g, carry):
+        by_lane = jnp.where(k == lo, 1.0, 0.0).astype(BF16)
+        oh_ref[pl.ds(pl.multiple_of(lax.rem(o + 8, TILES) * 128, 128), 128), :] = lax.dot_general(
+            identity, by_lane, NT, preferred_element_type=F32
+        ).astype(BF16)
+
+    def main_picks(q, carry):
+        for j in range(4):
+            picks(4 * q + j, codes_ref[4 * q + j, :, :128])
+        return carry
+
+    def rem_picks(q, carry):
         quarter = iota((1, 128), 1) // 32
-        code = codes_ref[4 * g, :, 128:]
-        for j in range(1, 4):
-            code = jnp.where(quarter == j, codes_ref[4 * g + j, :, 128:], code)
-        picks(32 + g, code)
-        return carry
-
-    lax.fori_loop(0, NF, main_picks, 0)
-    lax.fori_loop(0, 8, rem_picks, 0)
-
-    wait_far(0)
-    wait_near(0)
+        for j in range(4):
+            g = 4 * q + j
+            code = codes_ref[4 * g, :, 128:]
+            for e in range(1, 4):
+                code = jnp.where(quarter == e, codes_ref[4 * g + e, :, 128:], code)
+            picks(32 + g, code)
+        return carry
+
+    lax.fori_loop(0, NF // 4, main_picks, 0)
+    lax.fori_loop(0, 2, rem_picks, 0)
+
+    wait_one(0)
+    wait_group(0, 0)
+    wait_group(0, 1)
 
     def shuffle(g, carry):
         tiles = [rec_ref[0, 4 * g + j].astype(F32) for j in range(4)]
@@ -301,16 +306,11 @@
 
     rows = [part * 16 + r for part in range(2) for r in range(PAIRS)]
 
-    def first_tile(step):
-        late = jnp.where(step < 8, 4 * step, 4 * step - 32)
-        return jnp.where(step < 4, 8 + 4 * step, jnp.where(step < 6, 16 + 4 * step, late))
-
-    def spread(b4, step, lhs_ref):
+    def spread(b4, first, lhs_ref):
         for j in range(STEP):
-            o = first_tile(step) + j
-            at = pl.ds(pl.multiple_of(o * 128, 128), 128)
-            values = rec_ref[1 + b4, o].astype(F32)
-            picked = hm_ref[:, at]
+            tile = lax.rem(NF + first + j, TILES)
+            values = rec_ref[1 + b4, tile].astype(F32)
+            picked = hm_ref[:, pl.ds(pl.multiple_of(tile * 128, 128), 128)]
             lanes = slice(j * 128, j * 128 + 128)
             for i in range(PAIRS):
                 a = jnp.broadcast_to(values[rows[2 * i] : rows[2 * i] + 1], (8, 128))
@@ -322,37 +322,31 @@
                         * picked[16 * e : 16 * e + 16]
                     )
 
-    def place(step, lhs_ref, fresh):
-        at = pl.ds(pl.multiple_of(first_tile(step) * 128, 128), STEP * 128)
-        got = lax.dot_general(lhs_ref[...], oh_ref[:, at], NT, preferred_element_type=F32)
-        acc_ref[...] = got if fresh else acc_ref[...] + got
+    def place(first, lhs_ref):
+        at = pl.ds(pl.multiple_of(first * 128, 128), STEP * 128)
+        acc_ref[...] += jnp.dot(lhs_ref[...], oh_ref[at, :], preferred_element_type=F32)
 
     def stage(b4, carry):
-        wait_far(1 + b4)
-        spread(b4, 0, lhs_a)
+        wait_one(1 + b4)
         acc_ref[...] = jnp.zeros_like(acc_ref)
 
-        def two(i, c):
-            @pl.when(i == 2)
-            def _():
-                wait_near(1 + b4)
-
-            place(2 * i, lhs_a, False)
-            spread(b4, 2 * i + 1, lhs_b)
-            place(2 * i + 1, lhs_b, False)
-            spread(b4, jnp.minimum(2 * i + 2, STEPS - 1), lhs_a)
+        def half(i, c):
+            wait_group(1 + b4, i)
+            spread(b4, 20 * i, lhs_a)
+            place(20 * i, lhs_a)
+            spread(b4, 20 * i + 10, lhs_b)
+            place(20 * i + 10, lhs_b)
             return c
 
-        lax.fori_loop(0, STEPS // 2, two, 0)
+        lax.fori_loop(0, 2, half, 0)
         half_rows = PAIRS * HI
         g_ref[:, :256] = acc_ref[:half_rows].astype(BF16)
         g_ref[:, 256:] = acc_ref[half_rows:].astype(BF16)
+
         for block in range(6):
-            half = jnp.dot(
-                g_ref[...], rt_ref[:, block * 256 : (block + 1) * 256],
-                preferred_element_type=F32,
-            )
-            hs_ref[:, block * HI : (block + 1) * HI, :] = half.reshape(PAIRS, HI, 256)
+            at = slice(block * 256, (block + 1) * 256)
+            got = jnp.dot(g_ref[...], rt_ref[:, at], preferred_element_type=F32)
+            hs_ref[:, block * HI : (block + 1) * HI, :] = got.reshape(PAIRS, HI, 256)
         for p in range(PLANES):
             total = sum_ref[p]
             for bg in range(3):
@@ -443,7 +437,7 @@
             pltpu.VMEM((CHUNKS, NF, ROWS, 128), BF16),
             pltpu.VMEM((CHUNKS, TILES, ROWS, 128), BF16),
             pltpu.VMEM((48, KALL), BF16),
-            pltpu.VMEM((256, KALL), BF16),
+            pltpu.VMEM((KALL, 256), BF16),
             pltpu.VMEM((rows, STEP * 128), BF16),
             pltpu.VMEM((rows, STEP * 128), BF16),
             pltpu.VMEM((rows, 256), F32),
@@ -458,7 +452,7 @@
             pltpu.SemaphoreType.DMA,
             pltpu.SemaphoreType.DMA,
             pltpu.SemaphoreType.DMA((CHUNKS,)),
-            pltpu.SemaphoreType.DMA((CHUNKS, 2)),
+            pltpu.SemaphoreType.DMA((CHUNKS, 3)),
             pltpu.SemaphoreType.DMA,
             pltpu.SemaphoreType.DMA,
         ],

time: 56.5 us -> 54.8 us (0.970)
  Pallas kernels: 54.1 us -> 52.5 us
    pallas_call x1, Pallas kernels: 54.1 us -> 52.5 us  [shards(): pl.pallas_call(kernel, out_shape=jax.ShapeDtypeStruct((PLANES, XB, N), F3...]
where the time goes in v4:
time: 54.8 us; the launch traced here: 54.7 us
  Pallas kernels  52.5 us (96%)
  local copies, waits for them, and re-layouts  1.56 us (3%)
  between operations  0.66 us (1%)
    pallas_call x1, Pallas kernels, shards(): pl.pallas_call(kernel, out_shape=jax.ShapeDtypeStruct((PLANES, XB, N), F3...  52.5 us
    unnamed x1, local copies, waits for them, and re-layouts  1.56 us

profile of v4, /device:TPU:1, one launch (start us, length us, event | category | flops | bytes accessed | tf_op | source)
XLA Modules:
  0.0 54.7 jit_solution(3334652124116957608)
XLA Ops:
  0.7 52.5 %shard_map.82 = f32[5,18,144]{2,1,0:T(8,128)} custom-call(bf16[12,23040]{1,0:T(8,128)(2,1)} %x_hbm.1, bf16[288,256]{1,0:T(8,128)(2,1)} %constant.6.clone.trow_hbm, bf16[512,1536]{1,0:T(8,128)(2,1)} %constant.7.clone.rt_hbm, bf16[288,144]{1,0:T(8,128)(2,1)} %constant.8.clone.ct_hbm, s32[1,160]{1,0:T(1,128)} %bitcast.1, s32[160]{0:T(256)} %slot_ref.1, ...), custom_call_target="tpu_custom_call" | custom-call | tf_op jit(solution)/shard_map/pallas_call | solution.py:420
  53.1 1.6 %copy.11 = f32[5,18,144]{2,1,0:T(8,128)} copy(f32[5,18,144]{2,1,0:T(8,128)} %shard_map.82) | data formatting | bytes 103680

commit v5 on v4

--- a/solution.py
+++ b/solution.py
@@ -71,7 +71,12 @@
     return jnp.asarray(table.reshape(2 * N, 6 * HI), BF16)
 
 
-ORDER = [Y * dz + dy for dz in (0, 4, 3, 5, 2, 6, 1, 7) for dy in range(Y)]
+ORDER = [0] + [Y * dz + dy for dy in (2, 1, 3, 0) for dz in (1, 7, 2, 6, 3, 5, 4, 0)][:-1]
+
+
+FAR_FIRST = sorted(
+    range(1, NF), key=lambda o: -min(o // Y, Z - o // Y) - min(o % Y, Y - o % Y)
+)
 
 
 def iota(shape, dim):
@@ -81,10 +86,10 @@
 def kernel(
     x_hbm, trow_hbm, rt_hbm, ct_hbm, cols_ref, slot_ref, counts_ref, occ_ref,
     out_ref,
-    x_ref, trow_ref, rt_ref, ct_ref, xf_ref, xr_ref, chosen_ref, w_ref, xc_ref, code_ref, codes_ref,
+    x_ref, trow_ref, rt_ref, ct_ref, xf_ref, xr_ref, chosen_ref, w_ref, xc_ref, code_ref,
     send_ref, rec_ref, hm_ref, oh_ref, lhs_a, lhs_b, acc_ref,
     g_ref, hs_ref, sum_ref, stage_ref, bsend_ref, brec_ref, tot_ref,
-    ldsem, cssem, crsem, ssem, rsem, bssem, brsem,
+    ldsem, ssem, rsem, bssem, brsem,
 ):
     me = lax.axis_index("fft")
     band = lax.axis_index("band")
@@ -95,7 +100,7 @@
         return lax.rem(my_z + dz, Z) * Y + lax.rem(my_y + dy, Y)
 
     barrier = pltpu.get_barrier_semaphore()
-    for o in range(1, NF):
+    for o in FAR_FIRST:
         pl.semaphore_signal(barrier, inc=1, device_id=(peer(o), band), device_id_type=MESH)
     for o in range(1, NB):
         pl.semaphore_signal(
@@ -143,7 +148,14 @@
     gy = col - gx * GB
     natural = jnp.where(iota((16, SLOTS), 0) == 0, gx, gy).astype(BF16)
     ordered = jnp.dot(natural, order, preferred_element_type=F32)
-    code_ref[...] = ordered[0:1] * GB + ordered[1:2]
+    code = ordered[0:1] * GB + ordered[1:2]
+    high = jnp.floor(code * (1.0 / 64))
+    low = code - 64 * high
+    coded = (128 + high) * 2.0**-32
+    for bit in (32, 16, 8, 4, 2, 1):
+        coded = jnp.where(low >= bit, coded * 2.0**bit, coded)
+        low = jnp.where(low >= bit, low - bit, low)
+    code_ref[...] = coded
 
     loads[1].wait()
 
@@ -177,6 +189,7 @@
 
     lane = iota((1, 128), 1)
     count = counts_ref[0]
+    row32 = iota((ROWS, 128), 0)
 
     def outgoing(c):
         r = lax.rem(lane, 32)
@@ -185,7 +198,9 @@
         )
         live = jnp.where(slot < count, 1.0, 0.0)
         res = lax.dot_general(w_ref[...], xc_ref[c], NT, preferred_element_type=F32) * live
-        send_ref[c] = res.reshape(NF, ROWS, 128).astype(BF16)
+        codes = code_ref[...]
+        aux = jnp.where(row32 == 15, codes[:, :128], jnp.where(row32 == 31, codes[:, 128:], 0.0))
+        send_ref[c] = (res.reshape(NF, ROWS, 128) + aux[None]).astype(BF16)
 
     def block_copy(c, i):
         return pltpu.make_async_remote_copy(
@@ -213,21 +228,8 @@
     def wait_group(c, group):
         blocks(c, 1 + 16 * group, 15, group).wait_recv()
 
-    def code_copy(i):
-        return pltpu.make_async_remote_copy(
-            src_ref=code_ref,
-            dst_ref=codes_ref.at[i],
-            send_sem=cssem,
-            recv_sem=crsem,
-            device_id=(peer(ORDER[i]), band),
-            device_id_type=MESH,
-        )
-
     outgoing(0)
     pl.semaphore_wait(barrier, NF - 1 + NB - 1)
-    for i in range(1, NF):
-        code_copy(i).start()
-    codes_ref[0] = code_ref[...]
 
     def send_chunk(c, carry):
         @pl.when(c > 0)
@@ -243,19 +245,18 @@
 
     sum_ref[...] = jnp.zeros_like(sum_ref)
 
-    every_code = pltpu.make_async_remote_copy(
-        src_ref=codes_ref.at[pl.ds(1, NF - 1)],
-        dst_ref=codes_ref.at[pl.ds(1, NF - 1)],
-        send_sem=cssem,
-        recv_sem=crsem,
-        device_id=(peer(1), band),
-        device_id_type=MESH,
-    )
-    every_code.wait_recv()
-
+    wait_one(0)
+    wait_group(0, 0)
+    wait_group(0, 1)
     identity = jnp.where(iota((128, 128), 0) == iota((128, 128), 1), 1.0, 0.0).astype(BF16)
 
-    def picks(o, code):
+    def picks(o, coded):
+        high, code = coded * 2.0**32, jnp.zeros((1, 128), F32)
+        for bit in (32, 16, 8, 4, 2, 1):
+            above = high >= 128 * 2.0**bit
+            high = jnp.where(above, high * 2.0**-bit, high)
+            code = jnp.where(above, code + bit, code)
+        code += (high - 128) * 64
         at = pl.ds(pl.multiple_of(o * 128, 128), 128)
         hi = jnp.floor((code + 0.5) * (1.0 / (3 * GB)))
         lo = code - 3 * GB * hi
@@ -270,25 +271,22 @@
 
     def main_picks(q, carry):
         for j in range(4):
-            picks(4 * q + j, codes_ref[4 * q + j, :, :128])
+            picks(4 * q + j, rec_ref[0, 4 * q + j].astype(F32)[15:16])
         return carry
 
     def rem_picks(q, carry):
         quarter = iota((1, 128), 1) // 32
         for j in range(4):
             g = 4 * q + j
-            code = codes_ref[4 * g, :, 128:]
+            code = rec_ref[0, 4 * g].astype(F32)[31:32]
             for e in range(1, 4):
-                code = jnp.where(quarter == e, codes_ref[4 * g + e, :, 128:], code)
+                code = jnp.where(quarter == e, rec_ref[0, 4 * g + e].astype(F32)[31:32], code)
             picks(32 + g, code)
         return carry
 
     lax.fori_loop(0, NF // 4, main_picks, 0)
     lax.fori_loop(0, 2, rem_picks, 0)
 
-    wait_one(0)
-    wait_group(0, 0)
-    wait_group(0, 1)
 
     def shuffle(g, carry):
         tiles = [rec_ref[0, 4 * g + j].astype(F32) for j in range(4)]
@@ -409,7 +407,6 @@
     for p in range(PLANES):
         out_ref[p] = tot_ref[XB * p : XB * (p + 1), :N]
     band_blocks.wait_send()
-    every_code.wait_send()
 
 
 def shards(coefficients, occupations, columns, counts, plane_slot):
@@ -433,7 +430,6 @@
             pltpu.VMEM((NF * ROWS, 768), BF16),
             pltpu.VMEM((CHUNKS, 128, 768), BF16),
             pltpu.VMEM((1, 256), F32),
-            pltpu.VMEM((NF, 1, 256), F32),
             pltpu.VMEM((CHUNKS, NF, ROWS, 128), BF16),
             pltpu.VMEM((CHUNKS, TILES, ROWS, 128), BF16),
             pltpu.VMEM((48, KALL), BF16),
@@ -449,8 +445,6 @@
             pltpu.VMEM((NB, 112, 128), BF16),
             pltpu.VMEM((96, 256), F32),
             pltpu.SemaphoreType.DMA((4,)),
-            pltpu.SemaphoreType.DMA,
-            pltpu.SemaphoreType.DMA,
             pltpu.SemaphoreType.DMA((CHUNKS,)),
             pltpu.SemaphoreType.DMA((CHUNKS, 3)),
             pltpu.SemaphoreType.DMA,

time: 54.8 us -> 53.9 us (0.984)
  Pallas kernels: 52.5 us -> 51.6 us
    pallas_call x1, Pallas kernels: 52.5 us -> 51.6 us  [shards(): pl.pallas_call(kernel, out_shape=jax.ShapeDtypeStruct((PLANES, XB, N), F3...]
where the time goes in v5:
time: 53.9 us; the launch traced here: 53.8 us
  Pallas kernels  51.6 us (96%)
  local copies, waits for them, and re-layouts  1.56 us (3%)
  between operations  0.66 us (1%)
    pallas_call x1, Pallas kernels, shards(): pl.pallas_call(kernel, out_shape=jax.ShapeDtypeStruct((PLANES, XB, N), F3...  51.6 us
    unnamed x1, local copies, waits for them, and re-layouts  1.56 us

profile of v5, /device:TPU:1, one launch (start us, length us, event | category | flops | bytes accessed | tf_op | source)
XLA Modules:
  0.0 53.8 jit_solution(4775130212769218838)
XLA Ops:
  0.7 51.6 %shard_map.82 = f32[5,18,144]{2,1,0:T(8,128)} custom-call(bf16[12,23040]{1,0:T(8,128)(2,1)} %x_hbm.1, bf16[288,256]{1,0:T(8,128)(2,1)} %constant.6.clone.trow_hbm, bf16[512,1536]{1,0:T(8,128)(2,1)} %constant.7.clone.rt_hbm, bf16[288,144]{1,0:T(8,128)(2,1)} %constant.8.clone.ct_hbm, s32[1,160]{1,0:T(1,128)} %bitcast.1, s32[160]{0:T(256)} %slot_ref.1, ...), custom_call_target="tpu_custom_call" | custom-call | tf_op jit(solution)/shard_map/pallas_call | solution.py:417
  52.2 1.6 %copy.11 = f32[5,18,144]{2,1,0:T(8,128)} copy(f32[5,18,144]{2,1,0:T(8,128)} %shard_map.82) | data formatting | bytes 103680

commit v6 on v5

--- a/solution.py
+++ b/solution.py
@@ -185,7 +185,7 @@
                 xc_ref[1 + b4, 16 * t : 16 * t + 16, lanes] = value[:16].astype(BF16)
                 xr_ref[b4, 4 * t : 4 * t + 4, lanes] = value[16:20]
     for b4 in range(4):
-        xc_ref[0, 32 * b4 : 32 * b4 + 32, :] = xr_ref[b4].astype(BF16)
+        xc_ref[0, 32 * b4 : 32 * b4 + 32, :] = xr_ref[b4, :32].astype(BF16)
 
     lane = iota((1, 128), 1)
     count = counts_ref[0]
@@ -346,7 +346,7 @@
             got = jnp.dot(g_ref[...], rt_ref[:, at], preferred_element_type=F32)
             hs_ref[:, block * HI : (block + 1) * HI, :] = got.reshape(PAIRS, HI, 256)
         for p in range(PLANES):
-            total = sum_ref[p]
+            total = sum_ref[p, :N]
             for bg in range(3):
                 wave = jnp.dot(
                     ct_ref[...], hs_ref[bg * PLANES + p].astype(BF16),
@@ -354,7 +354,7 @@
                 )
                 re, im = wave[:N], wave[N:]
                 total += (re * re + im * im) * (occ_ref[bg * 4 + b4] * (1.0 / (BANDS_HERE * NB)))
-            sum_ref[p] = total
+            sum_ref[p, :N] = total
         return carry
 
     loads[2].wait()
@@ -372,7 +372,7 @@
             if i:
                 piece = pltpu.roll(piece, 16 * i, 1)
             extra = jnp.where(folded == i, piece, extra)
-        bsend_ref[j, :96] = stage_ref[j, :, :128].astype(BF16)
+        bsend_ref[j, :96] = stage_ref[j, :96, :128].astype(BF16)
         bsend_ref[j, 96:] = extra.astype(BF16)
     for o in range(1, NB):
         to = lax.rem(band + o, NB)
@@ -424,8 +424,8 @@
             pltpu.VMEM((2 * N, 256), BF16),
             pltpu.VMEM((512, 1536), BF16),
             pltpu.VMEM((2 * N, 6 * HI), BF16),
-            pltpu.VMEM((2880, 128), F32),
-            pltpu.VMEM((4, 32, 768), F32),
+            pltpu.VMEM((3456, 128), F32),
+            pltpu.VMEM((4, 40, 768), F32),
             pltpu.VMEM((NF * ROWS, 2 * N), BF16),
             pltpu.VMEM((NF * ROWS, 768), BF16),
             pltpu.VMEM((CHUNKS, 128, 768), BF16),
@@ -439,8 +439,8 @@
             pltpu.VMEM((rows, 256), F32),
             pltpu.VMEM((PAIRS * HI, 512), BF16),
             pltpu.VMEM((PAIRS, 6 * HI, 256), F32),
-            pltpu.VMEM((PLANES, N, 256), F32),
-            pltpu.VMEM((NB, 96, 256), F32),
+            pltpu.VMEM((PLANES, N + 8, 256), F32),
+            pltpu.VMEM((NB, 104, 256), F32),
             pltpu.VMEM((NB, 112, 128), BF16),
             pltpu.VMEM((NB, 112, 128), BF16),
             pltpu.VMEM((96, 256), F32),

time: 53.9 us -> 53.9 us (level)
  no operation moved by 1% of the time
where the time goes in v6:
time: 53.9 us; the launch traced here: 53.8 us
  Pallas kernels  51.6 us (96%)
  local copies, waits for them, and re-layouts  1.56 us (3%)
  between operations  0.66 us (1%)
    pallas_call x1, Pallas kernels, shards(): pl.pallas_call(kernel, out_shape=jax.ShapeDtypeStruct((PLANES, XB, N), F3...  51.6 us
    unnamed x1, local copies, waits for them, and re-layouts  1.56 us

profile of v6, /device:TPU:1, one launch (start us, length us, event | category | flops | bytes accessed | tf_op | source)
XLA Modules:
  0.0 53.8 jit_solution(17771815897234558674)
XLA Ops:
  0.7 51.6 %shard_map.82 = f32[5,18,144]{2,1,0:T(8,128)} custom-call(bf16[12,23040]{1,0:T(8,128)(2,1)} %x_hbm.1, bf16[288,256]{1,0:T(8,128)(2,1)} %constant.6.clone.trow_hbm, bf16[512,1536]{1,0:T(8,128)(2,1)} %constant.7.clone.rt_hbm, bf16[288,144]{1,0:T(8,128)(2,1)} %constant.8.clone.ct_hbm, s32[1,160]{1,0:T(1,128)} %bitcast.1, s32[160]{0:T(256)} %slot_ref.1, ...), custom_call_target="tpu_custom_call" | custom-call | tf_op jit(solution)/shard_map/pallas_call | solution.py:417
  52.2 1.6 %copy.11 = f32[5,18,144]{2,1,0:T(8,128)} copy(f32[5,18,144]{2,1,0:T(8,128)} %shard_map.82) | data formatting | bytes 103680
